TPU v7x, 32 devices: a whole 2x2x4 slice. The times are simulated.
32 devices in a mesh: group: 8 (over y, x, core), pos: 4 (over z).
Axes of the slice: x: 2, y: 2, z: 4, core: 2. Of those that a mesh axis runs over, the one named last changes fastest.
Arguments:
- features: bfloat16 [384, 256, 256], P(('group', 'pos')), may hold values from -6 to 6
- gain_attn: float32 [256], replicated, may hold values from 0.1 to 1.9
- w_query: bfloat16 [256, 256], replicated, as said below
- w_key: bfloat16 [256, 256], replicated, as said below
- w_value: bfloat16 [256, 256], replicated, may hold values from -0.375 to 0.375
- w_out: bfloat16 [256, 256], replicated, may hold values from -0.375 to 0.375
- gain_ffn: float32 [256], replicated, may hold values from 0.1 to 1.9
- w_up: bfloat16 [256, 1024], replicated, may hold values from -0.375 to 0.375
- w_down: bfloat16 [1024, 256], replicated, may hold values from -0.1875 to 0.1875
- counts: int32 [6], replicated, may hold values from 4 to 64, as said below
- offsets: int32 [6], replicated, may hold values from 0 to 380, as said below
Outputs:
- result: bfloat16 [384, 256, 256], P(('group', 'pos'))
Inputs may be any that keep to these rules, and one draw needn't show every extreme that they name: `counts`: each mixture has 4 to 64 groups, and one mixture has exactly 64. Mixture m occupies slots offsets[m] to offsets[m] + counts[m] - 1; the mixtures follow one another in order without intersection. `w_query`: a dense matrix of independent entries. `w_key`: a dense matrix of independent entries.
All inputs are finite; a program needn't handle non-finite values.
Results may differ from a plain program's by a relative error of at most 0.0065.
Values may be sent and summed in bfloat16 or wider, within the bound.
No kernel may reach another device: no remote copies, remote signals or barrier semaphores. Data moves between devices by JAX's collectives and lax.ppermute only.
A program may use at most 192 MiB of HBM per device.

v0:
```python
import math

import jax
import jax.numpy as jnp
from jax import lax
from jax.sharding import PartitionSpec as P

HEADS = 8


epsilon = 1e-05
masked_value = -1e30


def segment_ids(counts, offsets, slots_total):
    slots = jnp.arange(slots_total, dtype=jnp.int32)[:, None]
    inside = (slots >= offsets[None, :]) & (slots < offsets[None, :] + counts[None, :])
    labels = jnp.arange(counts.shape[0], dtype=jnp.int32)[None, :] + 1
    return jnp.sum(jnp.where(inside, labels, 0), axis=1) - 1


def layer_norm(values, gain):
    floats = values.astype(jnp.float32)
    average = jnp.mean(floats, axis=-1, keepdims=True)
    centred = floats - average
    spread = jnp.mean(centred * centred, axis=-1, keepdims=True)
    return (centred * lax.rsqrt(spread + epsilon) * gain).astype(jnp.bfloat16)


def feed_forward(middle, gain_ffn, w_up, w_down):
    second = layer_norm(middle, gain_ffn)
    hidden = jnp.maximum(jnp.dot(second, w_up, preferred_element_type=jnp.float32), 0.0).astype(
        jnp.bfloat16
    )
    return (
        middle.astype(jnp.float32) + jnp.dot(hidden, w_down, preferred_element_type=jnp.float32)
    ).astype(jnp.bfloat16)


def local(
    features, gain_attn, w_query, w_key, w_value, w_out, gain_ffn, w_up, w_down, counts, offsets
):
    group_devices = lax.axis_size("group")
    pos_devices = lax.axis_size("pos")
    local_groups = features.shape[0]
    width = features.shape[2]
    slots_total = local_groups * group_devices * pos_devices
    head_dim = width // HEADS
    scale = 1.0 / math.sqrt(head_dim)
    gathered = lax.all_to_all(features, ("group", "pos"), split_axis=1, concat_axis=0, tiled=True)
    owned = gathered.shape[1]
    labels = segment_ids(counts, offsets, slots_total)
    flat = gathered.reshape(slots_total * owned, width)
    normed = layer_norm(flat, gain_attn)

    def project(weight):
        product = jnp.dot(normed, weight, preferred_element_type=jnp.float32).astype(jnp.bfloat16)
        return product.reshape(slots_total, owned, HEADS, head_dim)

    query = project(w_query)
    keys = project(w_key)
    values = project(w_value)
    block = min(512, slots_total)

    def attend(start):
        block_query = lax.dynamic_slice_in_dim(query, start, block, 0)
        block_labels = lax.dynamic_slice_in_dim(labels, start, block, 0)
        scores = (
            jnp.einsum("qphe,kphe->phqk", block_query, keys, preferred_element_type=jnp.float32)
            * scale
        )
        allowed = (block_labels[:, None] == labels[None, :]) & (block_labels[:, None] >= 0)
        scores = jnp.where(allowed[None, None], scores, masked_value)
        highest = jnp.max(scores, axis=-1, keepdims=True)
        exponent = jnp.exp(scores - highest)
        total = jnp.sum(exponent, axis=-1, keepdims=True)
        weights = (exponent / total).astype(jnp.bfloat16)
        context = jnp.einsum(
            "phqk,kphe->qphe", weights, values, preferred_element_type=jnp.float32
        ).astype(jnp.bfloat16)
        return jnp.where((block_labels >= 0)[:, None, None, None], context, jnp.zeros_like(context))

    starts = jnp.arange(slots_total // block, dtype=jnp.int32) * block
    context = lax.map(attend, starts).reshape(slots_total * owned, width)
    middle = (
        flat.astype(jnp.float32) + jnp.dot(context, w_out, preferred_element_type=jnp.float32)
    ).astype(jnp.bfloat16)
    middle = middle.reshape(slots_total, owned, width)
    returned = lax.all_to_all(middle, ("group", "pos"), split_axis=0, concat_axis=1, tiled=True)
    finished = feed_forward(returned.reshape(-1, width), gain_ffn, w_up, w_down)
    return finished.reshape(returned.shape)


def solution(mesh):
    return jax.shard_map(
        local,
        mesh=mesh,
        in_specs=(
            P(("group", "pos"), None, None),
            P(),
            P(),
            P(),
            P(),
            P(),
            P(),
            P(),
            P(),
            P(),
            P(),
        ),
        out_specs=P(("group", "pos"), None, None),
        check_vma=False,
    )
```

profile of v0, /device:TPU:1, one launch (start us, length us, event | category | flops | bytes accessed | tf_op | source)
XLA Modules:
  0.0 253.2 jit_solution(11873321647180178728)
XLA Ops:
  0.0 0.0 copy-start
  0.0 0.0 copy-start.9
  0.0 0.0 copy-start.7
  0.0 3.7 %copy.33 = bf16[12,256,256]{2,0,1:T(8,128)(2,1)} copy(bf16[12,256,256]{2,1,0:T(8,128)(2,1)} %param.11) | data formatting | bytes 3145728 | tf_op args[0]
  3.8 7.1 %all-to-all-start = ((bf16[12,256,256]{2,0,1:T(8,128)(2,1)}), bf16[12,256,256]{2,0,1:T(8,128)(2,1)S(1)}, u32[]{:S(2)}, u32[]{:S(2)}) async-start(bf16[12,256,256]{2,0,1:T(8,128)(2,1)} %copy.33), calls=%async_computation | async-start | bytes 4194304 | tf_op jit(solution)/shard_map/all_to_all | solution.py:50
  10.8 0.0 copy-done.9
  10.9 0.0 copy-done.7
  10.9 0.1 select_reduce_fusion
  11.0 0.2 compare_and_fusion
  11.2 48.0 %all-to-all-done = bf16[12,256,256]{2,0,1:T(8,128)(2,1)S(1)} async-done(((bf16[12,256,256]{2,0,1:T(8,128)(2,1)}), bf16[12,256,256]{2,0,1:T(8,128)(2,1)S(1)}, u32[]{:S(2)}, u32[]{:S(2)}) %all-to-all-start) | async-done | bytes 1572896 | tf_op jit(solution)/shard_map/all_to_all | solution.py:50
  59.2 2.2 bitcast_reduce_fusion.1
  61.4 0.0 copy-start.5
  61.4 0.1 div.29
  61.5 2.8 %fusion.21 = f32[32,12,8]{2,1,0:T(8,128)S(1)} fusion(f32[12,32,8,256]{3,2,0,1:T(8,128)} %get-tuple-element.16, f32[32,12,8]{2,1,0:T(8,128)S(1)} %broadcast_multiply_fusion), kind=kLoop, calls=%fused_computation.36 | loop fusion | flops 2356224 | bytes 3170304 | tf_op jit(solution)/shard_map/reduce_sum | solution.py:26
  64.3 0.0 copy-start.1
  64.4 0.1 rsqrt.23
  64.5 0.0 copy-done.5
  64.5 3.1 %fusion.19 = bf16[3072,256]{1,0:T(8,128)(2,1)S(1)} fusion(f32[12,32,8,256]{3,2,0,1:T(8,128)} %get-tuple-element.16, f32[256]{0:T(256)S(1)} %copy-done.5, f32[3072]{0:T(1024)S(1)} %rsqrt.23, f32[3072]{0:T(1024)S(1)} %div.29), kind=kLoop, calls=%fused_computation.32 | loop fusion | flops 3145728 | bytes 4744192 | tf_op jit(solution)/shard_map/convert_element_type | solution.py:27
  67.6 0.0 copy-done.1
  67.6 1.7 convolution_convert_fusion.1
  69.4 0.0 copy-start.2
  69.4 7.9 %reshape.166 = bf16[384,8,8,32]{3,2,1,0:T(8,128)(2,1)} reshape(bf16[3072,256]{1,0:T(8,128)(2,1)} %convolution_convert_fusion.1) | data formatting | bytes 3145728 | tf_op jit(solution)/shard_map/reshape | solution.py:58
  77.2 0.0 copy-done.2
  77.2 1.7 convolution_convert_fusion
  78.9 7.9 %reshape.167 = bf16[384,8,8,32]{3,2,1,0:T(8,128)(2,1)} reshape(bf16[3072,256]{1,0:T(8,128)(2,1)} %convolution_convert_fusion) | data formatting | bytes 3145728 | tf_op jit(solution)/shard_map/reshape | solution.py:58
  86.8 0.0 copy-done.3
  86.8 1.7 convolution_convert_fusion.2
  88.5 7.9 %reshape.165 = bf16[384,8,8,32]{3,2,1,0:T(8,128)(2,1)} reshape(bf16[3072,256]{1,0:T(8,128)(2,1)} %convolution_convert_fusion.2) | data formatting | bytes 3145728 | tf_op jit(solution)/shard_map/reshape | solution.py:58
  96.4 22.9 %fusion.7 = f32[8,8,384,384]{2,3,1,0:T(8,128)} fusion(bf16[384,8,8,32]{3,2,1,0:T(8,128)(2,1)} %reshape.167, bf16[384,8,8,32]{3,2,1,0:T(8,128)(2,1)} %reshape.166), kind=kOutput, calls=%fused_computation.11 | convolution fusion | flops 603979776 | bytes 40894464 | tf_op jit(solution)/shard_map/while/body/eval_jaxpr/qphe,kphe->phqk/dot_general | solution.py:69
  119.3 42.9 %fusion.32 = (f32[8,8,384]{2,1,0:T(8,128)S(1)}, f32[8,8,384,384]{2,3,1,0:T(8,128)}) fusion(f32[8,8,384,384]{2,3,1,0:T(8,128)} %fusion.7, pred[384,384]{0,1:T(8,128)(4,1)S(1)} %compare_and_fusion), kind=kOutput, calls=%fused_computation.55 | output fusion | flops 56623488 | bytes 75743232 | tf_op jit(solution)/shard_map/while/body/eval_jaxpr/sub | solution.py:75
  162.3 17.4 %select_bitcast_fusion = bf16[384,8,8,32]{0,3,2,1:T(8,128)(2,1)S(1)} fusion(pred[384]{0:T(512)(128)(4,1)S(1)} %broadcast_compare_fusion, f32[8,8,384,384]{2,3,1,0:T(8,128)} %get-tuple-element.24, f32[8,8,384]{2,1,0:T(8,128)S(1)} %get-tuple-element.17, bf16[384,8,8,32]{3,2,1,0:T(8,128)(2,1)} %reshape.165), kind=kOutput, calls=%fused_computation.38 | convolution fusion | flops 624427008 | bytes 40993152 | tf_op jit(solution)/shard_map/while/body/eval_jaxpr/phqk,kphe->qphe/dot_general | solution.py:78
  179.7 9.3 %copy.39 = bf16[384,8,8,32]{3,2,1,0:T(8,128)(2,1)} copy(bf16[384,8,8,32]{0,3,2,1:T(8,128)(2,1)S(1)} %select_bitcast_fusion) | data formatting | bytes 3145728 | tf_op jit(solution)/shard_map/while/body/eval_jaxpr/jit(_where)/select_n | solution.py:81
  189.0 7.5 %reshape.168 = bf16[3072,256]{1,0:T(8,128)(2,1)S(1)} reshape(bf16[384,8,8,32]{3,2,1,0:T(8,128)(2,1)} %copy.39) | data formatting | bytes 3145728 | tf_op jit(solution)/shard_map/reshape | solution.py:84
  196.5 0.0 copy-done.4
  196.6 2.5 fusion.25
  199.0 40.7 %all_to_all.8 = bf16[384,8,256]{2,1,0:T(8,128)(2,1)S(1)} all-to-all(bf16[384,8,256]{2,1,0:T(8,128)(2,1)S(1)} %fusion.25), channel_id=1, replica_groups=mesh['group'=8,'pos'=4] {'group','pos'}, dimensions={0} | all-to-all | bytes 3145728 | tf_op jit(solution)/shard_map/all_to_all | solution.py:89
  239.7 0.5 bitcast_reduce_fusion
  240.2 0.0 copy-start.6
  240.2 2.0 copy.40
  242.2 0.9 fusion.16
  243.2 0.0 copy-start.8
  243.2 0.1 div.34
  243.4 0.1 rsqrt.25
  243.5 0.0 copy-done.6
  243.5 3.1 %fusion.14 = bf16[3072,256]{1,0:T(8,128)(2,1)S(1)} fusion(f32[32,12,8,256]{3,2,0,1:T(8,128)} %copy.40, f32[256]{0:T(256)S(1)} %copy-done.6, f32[3072]{0:T(1024)S(1)} %rsqrt.25, f32[3072]{0:T(1024)S(1)} %div.34), kind=kLoop, calls=%fused_computation.24 | loop fusion | flops 3145728 | bytes 4744192 | tf_op jit(solution)/shard_map/convert_element_type | solution.py:27
  246.6 0.0 copy-done
  246.6 0.0 copy-done.8
  246.6 6.6 %fusion.10 = bf16[3072,256]{1,0:T(8,128)(2,1)} fusion(f32[3072,256]{1,0:T(8,128)} %bitcast.58, bf16[1024,256]{1,0:T(8,128)(2,1)S(1)} %copy-done, bf16[3072,256]{1,0:T(8,128)(2,1)S(1)} %fusion.14, bf16[256,1024]{1,0:T(8,128)(2,1)S(1)} %copy-done.8), kind=kOutput, calls=%fused_computation.16 | convolution fusion | flops 3229089792 | bytes 7340032 | tf_op jit(solution)/shard_map/dot_general | solution.py:36
  (10 shorter events, 0.1 us)
Async XLA Ops:
  0.0 246.6 %copy-start = (bf16[1024,256]{1,0:T(8,128)(2,1)S(1)}, bf16[1024,256]{1,0:T(8,128)(2,1)}, u32[]{:S(2)}) copy-start(bf16[1024,256]{1,0:T(8,128)(2,1)} %param.19) | copy-start | bytes 1572868
  0.0 10.8 %copy-start.9 = (s32[6]{0:T(128)S(1)}, s32[6]{0:T(128)}, u32[]{:S(2)}) copy-start(s32[6]{0:T(128)} %param.20) | copy-start | bytes 76
  0.0 10.9 %copy-start.7 = (s32[6]{0:T(128)S(1)}, s32[6]{0:T(128)}, u32[]{:S(2)}) copy-start(s32[6]{0:T(128)} %param.21) | copy-start | bytes 76
  3.8 55.4 %all-to-all-start = ((bf16[12,256,256]{2,0,1:T(8,128)(2,1)}), bf16[12,256,256]{2,0,1:T(8,128)(2,1)S(1)}, u32[]{:S(2)}, u32[]{:S(2)}) async-start(bf16[12,256,256]{2,0,1:T(8,128)(2,1)} %copy.33), calls=%async_computation | async-start | bytes 4194304 | tf_op jit(solution)/shard_map/all_to_all | solution.py:50
  61.4 3.1 %copy-start.5 = (f32[256]{0:T(256)S(1)}, f32[256]{0:T(256)}, u32[]{:S(2)}) copy-start(f32[256]{0:T(256)} %param.12) | copy-start | bytes 3076
  64.3 3.3 %copy-start.1 = (bf16[256,256]{1,0:T(8,128)(2,1)S(1)}, bf16[256,256]{1,0:T(8,128)(2,1)}, u32[]{:S(2)}) copy-start(bf16[256,256]{1,0:T(8,128)(2,1)} %param.13) | copy-start | bytes 393220
  69.4 7.9 %copy-start.2 = (bf16[256,256]{1,0:T(8,128)(2,1)S(1)}, bf16[256,256]{1,0:T(8,128)(2,1)}, u32[]{:S(2)}) copy-start(bf16[256,256]{1,0:T(8,128)(2,1)} %param.14) | copy-start | bytes 393220
  78.9 7.9 %copy-start.3 = (bf16[256,256]{1,0:T(8,128)(2,1)S(1)}, bf16[256,256]{1,0:T(8,128)(2,1)}, u32[]{:S(2)}) copy-start(bf16[256,256]{1,0:T(8,128)(2,1)} %param.15) | copy-start | bytes 393220
  189.0 7.6 %copy-start.4 = (bf16[256,256]{1,0:T(8,128)(2,1)S(1)}, bf16[256,256]{1,0:T(8,128)(2,1)}, u32[]{:S(2)}) copy-start(bf16[256,256]{1,0:T(8,128)(2,1)} %param.16) | copy-start | bytes 393220
  240.2 3.3 %copy-start.6 = (f32[256]{0:T(256)S(1)}, f32[256]{0:T(256)}, u32[]{:S(2)}) copy-start(f32[256]{0:T(256)} %param.17) | copy-start | bytes 3076
  243.2 3.4 %copy-start.8 = (bf16[256,1024]{1,0:T(8,128)(2,1)S(1)}, bf16[256,1024]{1,0:T(8,128)(2,1)}, u32[]{:S(2)}) copy-start(bf16[256,1024]{1,0:T(8,128)(2,1)} %param.18) | copy-start | bytes 1572868
where the time goes:
time: 254 us; the launch traced here: 253 us
  other arithmetic  55.9 us (22%)
  matrix products  54.6 us (21%)
  waiting for transfers between devices  48 us (19%)
  local copies, waits for them, and re-layouts  46.7 us (18%)
  blocking collectives  40.7 us (16%)
  starting transfers between devices  7.08 us (3%)
    all_to_all x1, waiting for transfers between devices, local(): lax.all_to_all(features, ('group', 'pos'), split_axis=1, concat_axis=0, t...  48 us
    sub x1, other arithmetic, attend(): exponent = jnp.exp(scores - highest)  42.9 us
    all_to_all x1, blocking collectives, local(): lax.all_to_all(middle, ('group', 'pos'), split_axis=0, concat_axis=1, til...  40.7 us
    reshape x3, local copies, waits for them, and re-layouts, project(): return product.reshape(slots_total, owned, HEADS, head_dim)  23.6 us
    dot_general x1, matrix products, attend(): jnp.einsum('qphe,kphe->phqk', block_query, keys, preferred_element_type=j...  22.9 us
    dot_general x1, matrix products, attend(): jnp.einsum('phqk,kphe->qphe', weights, values, preferred_element_type=jnp...  17.4 us
    select_n x1, local copies, waits for them, and re-layouts, attend(): jnp.where((block_labels >= 0)[:, None, None, None], context, jnp.zeros_li...  9.28 us
    reshape x1, local copies, waits for them, and re-layouts, local(): context = lax.map(attend, starts).reshape(slots_total * owned, width)  7.55 us
  transfers between devices with their start and end apart: 1, of which 1 were waited for; matrix products, arithmetic and copies ran while one was open for 0% of the time, Pallas kernels for 0%

commit v1 on v0

v1 whole, which is shorter than its diff:
```python
import functools
import math

import jax
import jax.numpy as jnp
from jax import lax
from jax.experimental import pallas as pl
from jax.experimental.pallas import tpu as pltpu
from jax.sharding import PartitionSpec as P

HEADS = 8
LANES = 128


epsilon = 1e-05
masked_value = -1e30
f32 = jnp.float32
bf16 = jnp.bfloat16


def layer_norm(floats, gain):
    average = jnp.mean(floats, axis=-1, keepdims=True)
    centred = floats - average
    spread = jnp.mean(centred * centred, axis=-1, keepdims=True)
    return (centred * lax.rsqrt(spread + epsilon) * gain).astype(bf16)


def dot(a, b):
    return lax.dot_general(a, b, (((1,), (0,)), ((), ())), preferred_element_type=f32)


def dot_t(a, b):
    return lax.dot_general(a, b, (((1,), (1,)), ((), ())), preferred_element_type=f32)


def iota(shape, dim):
    return lax.broadcasted_iota(jnp.int32, shape, dim)


def attention_kernel(
    window,
    counts_ref,
    offsets_ref,
    x_ref,
    gain_ref,
    wq_ref,
    wk_ref,
    wv_ref,
    wo_ref,
    out_ref,
    q_ref,
    k_ref,
    v_ref,
    c_ref,
):
    slots, owned, width = x_ref.shape
    head_dim = width // HEADS
    mixtures = counts_ref.shape[0]
    span = min(window, max(1, 256 // owned))
    rows = span * owned
    chunks = window // span
    scale = math.log2(math.e) / math.sqrt(head_dim)
    across = max(1, min(HEADS, width // window))
    down = HEADS // across
    row, col = iota((rows, rows), 0), iota((rows, rows), 1)
    to_pos = ((row % span) * owned + row // span == col).astype(f32).astype(bf16)
    to_slot = ((col % span) * owned + col // span == row).astype(f32).astype(bf16)
    gain = gain_ref[...]
    lane = iota((window, width), 1) // head_dim
    in_down = [lane % down == j for j in range(down)]
    in_across = [lane // down == i for i in range(across)]
    key_at = iota((down * window, across * window), 1) % window
    slot_at = iota((rows, width), 0) // owned
    ones = (
        iota((across * window, width), 0) // window
        == iota((across * window, width), 1) // (head_dim * down)
    )
    ones = ones.astype(f32).astype(bf16)
    out_ref[...] = x_ref[...]

    def mixture(m, carry):
        begin, count = offsets_ref[m], counts_ref[m]
        start = jnp.minimum(begin, slots - window)
        low = begin - start
        high = low + count

        def taken(ref, c):
            return ref[pl.ds(start + c * span, span)].astype(f32).reshape(rows, width)

        for c in range(chunks):
            normed = dot(to_pos, layer_norm(taken(x_ref, c), gain)).astype(bf16)
            for weight, held in ((wq_ref, q_ref), (wk_ref, k_ref), (wv_ref, v_ref)):
                product = dot(normed, weight[...]).astype(bf16).astype(f32)
                for p in range(owned):
                    held[p, c * span : (c + 1) * span, :] = product[p * span : (p + 1) * span]

        live = (key_at >= low) & (key_at < high)
        for p in range(owned):
            query, keys, values = q_ref[p], k_ref[p], v_ref[p]
            query = jnp.concatenate([jnp.where(keep, query, 0.0) for keep in in_down], 0)
            keys = jnp.concatenate([jnp.where(keep, keys, 0.0) for keep in in_across], 0)
            values = jnp.concatenate([jnp.where(keep, values, 0.0) for keep in in_across], 0)
            scores = dot_t(query.astype(bf16), keys.astype(bf16)) * scale
            scores = jnp.where(live, scores, masked_value)
            parts = []
            step = max(LANES, window)
            for at in range(0, across * window, step):
                part = scores[:, at : at + step]
                if window >= step:
                    top = jnp.max(part, axis=-1, keepdims=True)
                else:
                    group = iota(part.shape, 1) // window
                    top = jnp.zeros_like(part)
                    for g in range(step // window):
                        best = jnp.max(
                            jnp.where(group == g, part, masked_value), axis=-1, keepdims=True
                        )
                        top = jnp.where(group == g, best, top)
                parts.append(jnp.exp2(part - top).astype(bf16))
            exponent = jnp.concatenate(parts, 1)
            total = dot(exponent, ones)
            context = dot(exponent, values.astype(bf16)) / total
            joined = context[:window]
            for j in range(1, down):
                joined = jnp.where(in_down[j], context[j * window : (j + 1) * window], joined)
            c_ref[p] = joined

        for c in range(chunks):
            context = jnp.concatenate(
                [c_ref[p, c * span : (c + 1) * span, :] for p in range(owned)], 0
            ).astype(bf16)
            context = dot(to_slot, context).astype(bf16)
            middle = taken(x_ref, c) + dot(context, wo_ref[...])
            at = slot_at + c * span
            middle = jnp.where((at >= low) & (at < high), middle, taken(out_ref, c))
            out_ref[pl.ds(start + c * span, span)] = middle.reshape(span, owned, width).astype(bf16)
        return carry

    lax.fori_loop(0, mixtures, mixture, 0)


def attention(gathered, gain, w_query, w_key, w_value, w_out, counts, offsets):
    slots, owned, width = gathered.shape
    window = slots // counts.shape[0]
    vmem = pl.BlockSpec(memory_space=pltpu.VMEM)
    smem = pl.BlockSpec(memory_space=pltpu.SMEM)
    held = pltpu.VMEM((owned, window, width), f32)
    return pl.pallas_call(
        functools.partial(attention_kernel, window),
        out_shape=jax.ShapeDtypeStruct(gathered.shape, bf16),
        in_specs=[smem, smem] + [vmem] * 6,
        out_specs=vmem,
        scratch_shapes=[held] * 4,
        compiler_params=pltpu.CompilerParams(vmem_limit_bytes=48 * 1024 * 1024),
        cost_estimate=pl.CostEstimate(
            flops=14 * 10**9, bytes_accessed=2 * gathered.size * 2, transcendentals=10**6
        ),
        name="attention",
    )(counts, offsets, gathered, gain, w_query, w_key, w_value, w_out)


def feed_forward_kernel(each, x_ref, gain_ref, up_ref, down_ref, out_ref):
    width = x_ref.shape[-1]
    gain = gain_ref[...]
    for s in range(out_ref.shape[0]):
        middle = x_ref[:, s * each : (s + 1) * each, :].astype(f32).reshape(-1, width)
        second = layer_norm(middle, gain)
        hidden = jnp.maximum(dot(second, up_ref[...]), 0.0).astype(bf16)
        out_ref[s] = (middle + dot(hidden, down_ref[...])).astype(bf16)


def feed_forward(middle, groups, gain, w_up, w_down):
    devices, rows, width = middle.shape
    each = rows // groups
    if each % 8:
        middle = middle.reshape(devices, groups, each, width).swapaxes(0, 1)
        middle = middle.reshape(1, groups * devices * each, width)
        devices, each = 1, devices * each
    block = 4 if groups % 4 == 0 else 1
    whole = lambda shape: pl.BlockSpec(shape, lambda s: (0,) * len(shape))
    return pl.pallas_call(
        functools.partial(feed_forward_kernel, each),
        out_shape=jax.ShapeDtypeStruct((groups, devices * each, width), bf16),
        grid=(groups // block,),
        in_specs=[
            pl.BlockSpec((devices, block * each, width), lambda s: (0, s, 0)),
            whole(gain.shape),
            whole(w_up.shape),
            whole(w_down.shape),
        ],
        out_specs=pl.BlockSpec((block, devices * each, width), lambda s: (s, 0, 0)),
        compiler_params=pltpu.CompilerParams(vmem_limit_bytes=48 * 1024 * 1024),
        cost_estimate=pl.CostEstimate(
            flops=4 * middle.size * w_up.shape[1], bytes_accessed=4 * middle.size, transcendentals=0
        ),
        name="feed_forward",
    )(middle, gain, w_up, w_down)


def local(
    features, gain_attn, w_query, w_key, w_value, w_out, gain_ffn, w_up, w_down, counts, offsets
):
    axes = ("group", "pos")
    devices = lax.axis_size("group") * lax.axis_size("pos")
    groups, positions, width = features.shape
    owned = positions // devices
    slots = groups * devices
    sent = features.reshape(groups, devices, owned, width).swapaxes(0, 1)
    sent = sent.reshape(slots, owned, width)
    gathered = lax.all_to_all(sent, axes, split_axis=0, concat_axis=0, tiled=True)
    middle = attention(
        gathered, gain_attn.reshape(1, width), w_query, w_key, w_value, w_out, counts, offsets
    )
    returned = lax.all_to_all(middle, axes, split_axis=0, concat_axis=0, tiled=True)
    returned = returned.reshape(devices, groups * owned, width)
    return feed_forward(returned, groups, gain_ffn.reshape(1, width), w_up, w_down)


def solution(mesh):
    return jax.shard_map(
        local,
        mesh=mesh,
        in_specs=(P(("group", "pos"), None, None),) + (P(),) * 10,
        out_specs=P(("group", "pos"), None, None),
        check_vma=False,
    )
```

time: 254 us -> 107 us (0.42)
  other arithmetic: 55.9 us -> 0 us
  matrix products: 54.6 us -> 0 us
  waiting for transfers between devices: 48 us -> 0 us
  local copies, waits for them, and re-layouts: 46.7 us -> 1.65 us
  blocking collectives: 40.7 us -> 85.3 us
  Pallas kernels: 0 us -> 20.1 us
  starting transfers between devices: 7.08 us -> 0 us
    dot_general x7 -> x0, matrix products: 54.6 us -> none  [the longest x1 22.9 us: attend(): jnp.einsum('qphe,kphe->phqk', block_query, keys, preferred_element_type=j...]
    all_to_all x1 -> x0, waiting for transfers between devices: 48 us -> none  [local(): lax.all_to_all(features, ('group', 'pos'), split_axis=1, concat_axis=0, t...]
    all_to_all x1 -> x2, blocking collectives: 40.7 us -> 85.3 us  [the longest x1 44.6 us: local(): lax.all_to_all(sent, axes, split_axis=0, concat_axis=0, tiled=True)]
    sub x2 -> x0, other arithmetic: 42.9 us -> none  [the longest x1 42.9 us: attend(): exponent = jnp.exp(scores - highest)]
    reshape x4 -> x1, local copies, waits for them, and re-layouts: 31.2 us -> 1.59 us  [local(): sent = features.reshape(groups, devices, owned, width).swapaxes(0, 1)]
    pallas_call x0 -> x2, Pallas kernels: none -> 20.1 us  [the longest x1 14.4 us: attention(): pl.pallas_call(functools.partial(attention_kernel, window), out_shape=jax...]
    select_n x1 -> x0, local copies, waits for them, and re-layouts: 9.28 us -> none  [attend(): jnp.where((block_labels >= 0)[:, None, None, None], context, jnp.zeros_li...]
    all_to_all x1 -> x0, starting transfers between devices: 7.08 us -> none  [local(): lax.all_to_all(features, ('group', 'pos'), split_axis=1, concat_axis=0, t...]
  transfers between devices with their start and end apart: 1 -> 0, of which waited for: 1 -> 0; matrix products, arithmetic and copies ran while one was open for 0% -> 0% of each run, Pallas kernels for 0% -> 0%
where the time goes in v1:
time: 107 us
  blocking collectives  85.3 us (80%)
  Pallas kernels  20.1 us (19%)
  local copies, waits for them, and re-layouts  1.65 us (2%)
    all_to_all x1, blocking collectives, local(): lax.all_to_all(sent, axes, split_axis=0, concat_axis=0, tiled=True)  44.6 us
    all_to_all x1, blocking collectives, local(): lax.all_to_all(middle, axes, split_axis=0, concat_axis=0, tiled=True)  40.7 us
    pallas_call x1, Pallas kernels, attention(): pl.pallas_call(functools.partial(attention_kernel, window), out_shape=jax...  14.4 us
    pallas_call x1, Pallas kernels, feed_forward(): pl.pallas_call(functools.partial(feed_forward_kernel, each), out_shape=ja...  5.71 us

profile of v1, /device:TPU:1, one launch (start us, length us, event | category | flops | bytes accessed | tf_op | source)
XLA Modules:
  0.0 107.2 jit_solution(15257226081658798909)
XLA Ops:
  0.0 1.6 %copy.12 = bf16[12,32,8,256]{3,2,0,1:T(8,128)(2,1)S(1)} copy(bf16[12,32,8,256]{3,2,1,0:T(8,128)(2,1)} %bitcast.11) | data formatting | bytes 3145728 | tf_op jit(solution)/shard_map/reshape | solution.py:208
  1.6 0.0 copy-start.2
  1.6 0.0 copy-start.3
  1.6 0.0 copy-start.4
  1.6 0.0 copy-start.5
  1.6 0.0 copy-start.6
  1.7 0.0 copy-start.8
  1.7 0.0 copy-start.9
  1.7 44.6 %all_to_all.10.x_ref = bf16[384,8,256]{2,1,0:T(8,128)(2,1)S(1)} all-to-all(bf16[384,8,256]{2,1,0:T(8,128)(2,1)S(1)} %bitcast.10), channel_id=1, replica_groups=mesh['group'=8,'pos'=4] {'group','pos'}, dimensions={0} | all-to-all | bytes 3145728 | tf_op jit(solution)/shard_map/all_to_all | solution.py:210
  46.3 0.0 copy-done.2
  46.3 0.0 copy-done.3
  46.3 0.0 copy-done.4
  46.3 0.0 copy-done.5
  46.3 0.0 copy-done.6
  46.3 0.0 copy-done.8
  46.4 0.0 copy-done.9
  46.4 14.4 %attention.1 = bf16[384,8,256]{2,1,0:T(8,128)(2,1)S(1)} custom-call(s32[6]{0:T(128)S(1)} %copy-done.8, s32[6]{0:T(128)S(1)} %copy-done.9, bf16[384,8,256]{2,1,0:T(8,128)(2,1)S(1)} %all_to_all.10.x_ref, f32[1,256]{1,0:T(1,128)S(1)} %bitcast.8, bf16[256,256]{1,0:T(8,128)(2,1)S(1)} %copy-done.2, bf16[256,256]{1,0:T(8,128)(2,1)S(1)} %copy-done.3, ...), custom_call_target="tpu_custom_call" | custom-call | flops 14000000000 | bytes 3145728 | tf_op jit(solution)/shard_map/attention/pallas_call | solution.py:148
  60.8 0.0 copy-start
  60.8 0.0 copy-start.1
  60.8 0.0 copy-start.7
  60.8 40.7 %all_to_all.11 = bf16[384,8,256]{2,1,0:T(8,128)(2,1)S(1)} all-to-all(bf16[384,8,256]{2,1,0:T(8,128)(2,1)S(1)} %attention.1), channel_id=1, replica_groups=mesh['group'=8,'pos'=4] {'group','pos'}, dimensions={0} | all-to-all | bytes 3145728 | tf_op jit(solution)/shard_map/all_to_all | solution.py:214
  101.5 0.0 copy-done
  101.5 0.0 copy-done.1
  101.5 0.0 copy-done.7
  101.5 5.7 %feed_forward.1 = bf16[12,256,256]{2,1,0:T(8,128)(2,1)} custom-call(bf16[32,96,256]{2,1,0:T(8,128)(2,1)S(1)} %bitcast.7, f32[1,256]{1,0:T(1,128)S(1)} %bitcast.9, bf16[256,1024]{1,0:T(8,128)(2,1)S(1)} %copy-done, bf16[1024,256]{1,0:T(8,128)(2,1)S(1)} %copy-done.1), custom_call_target="tpu_custom_call" | custom-call | flops 3221225472 | bytes 3145728 | tf_op jit(solution)/shard_map/feed_forward/pallas_call | solution.py:181
Async XLA Ops:
  1.6 44.7 %copy-start.2 = (bf16[256,256]{1,0:T(8,128)(2,1)S(1)}, bf16[256,256]{1,0:T(8,128)(2,1)}, u32[]{:S(2)}) copy-start(bf16[256,256]{1,0:T(8,128)(2,1)} %wq_ref.1) | copy-start | bytes 393220
  1.6 44.7 %copy-start.3 = (bf16[256,256]{1,0:T(8,128)(2,1)S(1)}, bf16[256,256]{1,0:T(8,128)(2,1)}, u32[]{:S(2)}) copy-start(bf16[256,256]{1,0:T(8,128)(2,1)} %wk_ref.1) | copy-start | bytes 393220
  1.6 44.7 %copy-start.4 = (bf16[256,256]{1,0:T(8,128)(2,1)S(1)}, bf16[256,256]{1,0:T(8,128)(2,1)}, u32[]{:S(2)}) copy-start(bf16[256,256]{1,0:T(8,128)(2,1)} %wv_ref.1) | copy-start | bytes 393220
  1.6 44.7 %copy-start.5 = (bf16[256,256]{1,0:T(8,128)(2,1)S(1)}, bf16[256,256]{1,0:T(8,128)(2,1)}, u32[]{:S(2)}) copy-start(bf16[256,256]{1,0:T(8,128)(2,1)} %wo_ref.1) | copy-start | bytes 393220
  1.6 44.7 %copy-start.6 = (f32[256]{0:T(256)S(1)}, f32[256]{0:T(256)}, u32[]{:S(2)}) copy-start(f32[256]{0:T(256)} %param.12) | copy-start | bytes 3076
  1.7 44.7 %copy-start.8 = (s32[6]{0:T(128)S(1)}, s32[6]{0:T(128)}, u32[]{:S(2)}) copy-start(s32[6]{0:T(128)} %counts_ref.1) | copy-start | bytes 76
  1.7 44.7 %copy-start.9 = (s32[6]{0:T(128)S(1)}, s32[6]{0:T(128)}, u32[]{:S(2)}) copy-start(s32[6]{0:T(128)} %offsets_ref.1) | copy-start | bytes 76
  60.8 40.7 %copy-start = (bf16[256,1024]{1,0:T(8,128)(2,1)S(1)}, bf16[256,1024]{1,0:T(8,128)(2,1)}, u32[]{:S(2)}) copy-start(bf16[256,1024]{1,0:T(8,128)(2,1)} %up_ref.1) | copy-start | bytes 1572868
  60.8 40.7 %copy-start.1 = (bf16[1024,256]{1,0:T(8,128)(2,1)S(1)}, bf16[1024,256]{1,0:T(8,128)(2,1)}, u32[]{:S(2)}) copy-start(bf16[1024,256]{1,0:T(8,128)(2,1)} %down_ref.1) | copy-start | bytes 1572868
  60.8 40.7 %copy-start.7 = (f32[256]{0:T(256)S(1)}, f32[256]{0:T(256)}, u32[]{:S(2)}) copy-start(f32[256]{0:T(256)} %param.17) | copy-start | bytes 3076

commit v2 on v1

--- a/solution.py
+++ b/solution.py
@@ -48,10 +48,7 @@
     wv_ref,
     wo_ref,
     out_ref,
-    q_ref,
-    k_ref,
-    v_ref,
-    c_ref,
+    *held,
 ):
     slots, owned, width = x_ref.shape
     head_dim = width // HEADS
@@ -69,74 +66,91 @@
     lane = iota((window, width), 1) // head_dim
     in_down = [lane % down == j for j in range(down)]
     in_across = [lane // down == i for i in range(across)]
-    key_at = iota((down * window, across * window), 1) % window
     slot_at = iota((rows, width), 0) // owned
-    ones = (
-        iota((across * window, width), 0) // window
-        == iota((across * window, width), 1) // (head_dim * down)
-    )
+    pooled = (across * window, width)
+    ones = iota(pooled, 0) // window == iota(pooled, 1) // (head_dim * down)
     ones = ones.astype(f32).astype(bf16)
+    none = jnp.zeros((window, width), bf16)
     out_ref[...] = x_ref[...]
 
-    def mixture(m, carry):
-        begin, count = offsets_ref[m], counts_ref[m]
+    def place(m):
+        m = jnp.clip(m, 0, mixtures - 1)
+        begin = offsets_ref[m]
         start = jnp.minimum(begin, slots - window)
-        low = begin - start
-        high = low + count
-
-        def taken(ref, c):
-            return ref[pl.ds(start + c * span, span)].astype(f32).reshape(rows, width)
-
+        return start, begin - start, begin - start + counts_ref[m]
+
+    def taken(ref, start, c):
+        return ref[pl.ds(start + c * span, span)].astype(f32).reshape(rows, width)
+
+    def project(m, q_ref, k_ref, v_ref, c_ref):
+        start, _, _ = place(m)
         for c in range(chunks):
-            normed = dot(to_pos, layer_norm(taken(x_ref, c), gain)).astype(bf16)
+            normed = dot(to_pos, layer_norm(taken(x_ref, start, c), gain)).astype(bf16)
             for weight, held in ((wq_ref, q_ref), (wk_ref, k_ref), (wv_ref, v_ref)):
-                product = dot(normed, weight[...]).astype(bf16).astype(f32)
+                product = dot(normed, weight[...])
+                if held is q_ref:
+                    product = product * scale
+                product = product.astype(bf16)
                 for p in range(owned):
                     held[p, c * span : (c + 1) * span, :] = product[p * span : (p + 1) * span]
 
-        live = (key_at >= low) & (key_at < high)
+    def stacked(values, masks):
+        return jnp.concatenate([jnp.where(mask, values, none) for mask in masks], 0)
+
+    def join(parts):
+        joined = parts[:window]
+        for j in range(1, down):
+            joined = jnp.where(in_down[j], parts[j * window : (j + 1) * window], joined)
+        return joined
+
+    def attend(m, q_ref, k_ref, v_ref, c_ref):
+        _, low, high = place(m)
+        step = max(LANES, window)
+        key_at = iota((down * window, step), 1)
+        group = key_at // window
+        live = (key_at % window >= low) & (key_at % window < high)
+        masks = [live & (group == g) for g in range(step // window)]
         for p in range(owned):
-            query, keys, values = q_ref[p], k_ref[p], v_ref[p]
-            query = jnp.concatenate([jnp.where(keep, query, 0.0) for keep in in_down], 0)
-            keys = jnp.concatenate([jnp.where(keep, keys, 0.0) for keep in in_across], 0)
-            values = jnp.concatenate([jnp.where(keep, values, 0.0) for keep in in_across], 0)
-            scores = dot_t(query.astype(bf16), keys.astype(bf16)) * scale
-            scores = jnp.where(live, scores, masked_value)
+            scores = dot_t(stacked(q_ref[p], in_down), stacked(k_ref[p], in_across))
             parts = []
-            step = max(LANES, window)
             for at in range(0, across * window, step):
                 part = scores[:, at : at + step]
-                if window >= step:
-                    top = jnp.max(part, axis=-1, keepdims=True)
-                else:
-                    group = iota(part.shape, 1) // window
-                    top = jnp.zeros_like(part)
-                    for g in range(step // window):
-                        best = jnp.max(
-                            jnp.where(group == g, part, masked_value), axis=-1, keepdims=True
-                        )
-                        top = jnp.where(group == g, best, top)
-                parts.append(jnp.exp2(part - top).astype(bf16))
+                top = None
+                for g, mask in enumerate(masks):
+                    best = jnp.max(jnp.where(mask, part, masked_value), axis=-1, keepdims=True)
+                    top = best if top is None else jnp.where(group == g, best, top)
+                parts.append(jnp.exp2(jnp.where(live, part - top, masked_value)).astype(bf16))
             exponent = jnp.concatenate(parts, 1)
-            total = dot(exponent, ones)
-            context = dot(exponent, values.astype(bf16)) / total
-            joined = context[:window]
-            for j in range(1, down):
-                joined = jnp.where(in_down[j], context[j * window : (j + 1) * window], joined)
-            c_ref[p] = joined
-
+            total = join(dot(exponent, ones))
+            c_ref[p] = join(dot(exponent, stacked(v_ref[p], in_across))) / total
+
+    def finish(m, q_ref, k_ref, v_ref, c_ref):
+        start, low, high = place(m)
+        high = jnp.where(m < 0, low, high)
         for c in range(chunks):
             context = jnp.concatenate(
                 [c_ref[p, c * span : (c + 1) * span, :] for p in range(owned)], 0
             ).astype(bf16)
             context = dot(to_slot, context).astype(bf16)
-            middle = taken(x_ref, c) + dot(context, wo_ref[...])
+            middle = taken(x_ref, start, c) + dot(context, wo_ref[...])
             at = slot_at + c * span
-            middle = jnp.where((at >= low) & (at < high), middle, taken(out_ref, c))
+            middle = jnp.where((at >= low) & (at < high), middle, taken(out_ref, start, c))
             out_ref[pl.ds(start + c * span, span)] = middle.reshape(span, owned, width).astype(bf16)
+
+    even, odd = held[:4], held[4:]
+    odd[3][...] = jnp.zeros(odd[3].shape, f32)
+    project(0, *even)
+
+    def pair(i, carry):
+        m = 2 * i
+        for now, this, other in ((m, even, odd), (m + 1, odd, even)):
+            finish(now - 1, *other)
+            attend(now, *this)
+            project(now + 1, *other)
         return carry
 
-    lax.fori_loop(0, mixtures, mixture, 0)
+    lax.fori_loop(0, pl.cdiv(mixtures, 2), pair, 0)
+    finish(2 * pl.cdiv(mixtures, 2) - 1, *odd)
 
 
 def attention(gathered, gain, w_query, w_key, w_value, w_out, counts, offsets):
@@ -144,13 +158,13 @@
     window = slots // counts.shape[0]
     vmem = pl.BlockSpec(memory_space=pltpu.VMEM)
     smem = pl.BlockSpec(memory_space=pltpu.SMEM)
-    held = pltpu.VMEM((owned, window, width), f32)
+    held = pltpu.VMEM((owned, window, width), bf16)
     return pl.pallas_call(
         functools.partial(attention_kernel, window),
         out_shape=jax.ShapeDtypeStruct(gathered.shape, bf16),
         in_specs=[smem, smem] + [vmem] * 6,
         out_specs=vmem,
-        scratch_shapes=[held] * 4,
+        scratch_shapes=([held] * 3 + [pltpu.VMEM((owned, window, width), f32)]) * 2,
         compiler_params=pltpu.CompilerParams(vmem_limit_bytes=48 * 1024 * 1024),
         cost_estimate=pl.CostEstimate(
             flops=14 * 10**9, bytes_accessed=2 * gathered.size * 2, transcendentals=10**6

time: 107 us -> 104 us (0.972)
  Pallas kernels: 20.1 us -> 17 us
    pallas_call x1, Pallas kernels: 14.4 us -> 11.3 us  [attention(): pl.pallas_call(functools.partial(attention_kernel, window), out_shape=jax...]
where the time goes in v2:
time: 104 us
  blocking collectives  85.3 us (82%)
  Pallas kernels  17 us (16%)
  local copies, waits for them, and re-layouts  1.65 us (2%)
    all_to_all x1, blocking collectives, local(): lax.all_to_all(sent, axes, split_axis=0, concat_axis=0, tiled=True)  44.6 us
    all_to_all x1, blocking collectives, local(): lax.all_to_all(middle, axes, split_axis=0, concat_axis=0, tiled=True)  40.7 us
    pallas_call x1, Pallas kernels, attention(): pl.pallas_call(functools.partial(attention_kernel, window), out_shape=jax...  11.3 us
    pallas_call x1, Pallas kernels, feed_forward(): pl.pallas_call(functools.partial(feed_forward_kernel, each), out_shape=ja...  5.7 us

profile of v2, /device:TPU:1, one launch (start us, length us, event | category | flops | bytes accessed | tf_op | source)
XLA Modules:
  0.0 104.1 jit_solution(11355298930261297499)
XLA Ops:
  0.0 1.6 %copy.12 = bf16[12,32,8,256]{3,2,0,1:T(8,128)(2,1)S(1)} copy(bf16[12,32,8,256]{3,2,1,0:T(8,128)(2,1)} %bitcast.11) | data formatting | bytes 3145728 | tf_op jit(solution)/shard_map/reshape | solution.py:222
  1.6 0.0 copy-start.2
  1.6 0.0 copy-start.3
  1.6 0.0 copy-start.4
  1.6 0.0 copy-start.5
  1.6 0.0 copy-start.6
  1.7 0.0 copy-start.8
  1.7 0.0 copy-start.9
  1.7 44.6 %all_to_all.10.x_ref = bf16[384,8,256]{2,1,0:T(8,128)(2,1)S(1)} all-to-all(bf16[384,8,256]{2,1,0:T(8,128)(2,1)S(1)} %bitcast.10), channel_id=1, replica_groups=mesh['group'=8,'pos'=4] {'group','pos'}, dimensions={0} | all-to-all | bytes 3145728 | tf_op jit(solution)/shard_map/all_to_all | solution.py:224
  46.3 0.0 copy-done.2
  46.3 0.0 copy-done.3
  46.3 0.0 copy-done.4
  46.3 0.0 copy-done.5
  46.3 0.0 copy-done.6
  46.3 0.0 copy-done.8
  46.4 0.0 copy-done.9
  46.4 11.3 %attention.1 = bf16[384,8,256]{2,1,0:T(8,128)(2,1)S(1)} custom-call(s32[6]{0:T(128)S(1)} %copy-done.8, s32[6]{0:T(128)S(1)} %copy-done.9, bf16[384,8,256]{2,1,0:T(8,128)(2,1)S(1)} %all_to_all.10.x_ref, f32[1,256]{1,0:T(1,128)S(1)} %bitcast.8, bf16[256,256]{1,0:T(8,128)(2,1)S(1)} %copy-done.2, bf16[256,256]{1,0:T(8,128)(2,1)S(1)} %copy-done.3, ...), custom_call_target="tpu_custom_call" | custom-call | flops 14000000000 | bytes 3145728 | tf_op jit(solution)/shard_map/attention/pallas_call | solution.py:162
  57.7 0.0 copy-start
  57.7 0.0 copy-start.1
  57.7 0.0 copy-start.7
  57.7 40.7 %all_to_all.11 = bf16[384,8,256]{2,1,0:T(8,128)(2,1)S(1)} all-to-all(bf16[384,8,256]{2,1,0:T(8,128)(2,1)S(1)} %attention.1), channel_id=1, replica_groups=mesh['group'=8,'pos'=4] {'group','pos'}, dimensions={0} | all-to-all | bytes 3145728 | tf_op jit(solution)/shard_map/all_to_all | solution.py:228
  98.4 0.0 copy-done
  98.4 0.0 copy-done.1
  98.4 0.0 copy-done.7
  98.4 5.7 %feed_forward.1 = bf16[12,256,256]{2,1,0:T(8,128)(2,1)} custom-call(bf16[32,96,256]{2,1,0:T(8,128)(2,1)S(1)} %bitcast.7, f32[1,256]{1,0:T(1,128)S(1)} %bitcast.9, bf16[256,1024]{1,0:T(8,128)(2,1)S(1)} %copy-done, bf16[1024,256]{1,0:T(8,128)(2,1)S(1)} %copy-done.1), custom_call_target="tpu_custom_call" | custom-call | flops 3221225472 | bytes 3145728 | tf_op jit(solution)/shard_map/feed_forward/pallas_call | solution.py:195
Async XLA Ops:
  1.6 44.7 %copy-start.2 = (bf16[256,256]{1,0:T(8,128)(2,1)S(1)}, bf16[256,256]{1,0:T(8,128)(2,1)}, u32[]{:S(2)}) copy-start(bf16[256,256]{1,0:T(8,128)(2,1)} %wq_ref.1) | copy-start | bytes 393220
  1.6 44.7 %copy-start.3 = (bf16[256,256]{1,0:T(8,128)(2,1)S(1)}, bf16[256,256]{1,0:T(8,128)(2,1)}, u32[]{:S(2)}) copy-start(bf16[256,256]{1,0:T(8,128)(2,1)} %wk_ref.1) | copy-start | bytes 393220
  1.6 44.7 %copy-start.4 = (bf16[256,256]{1,0:T(8,128)(2,1)S(1)}, bf16[256,256]{1,0:T(8,128)(2,1)}, u32[]{:S(2)}) copy-start(bf16[256,256]{1,0:T(8,128)(2,1)} %wv_ref.1) | copy-start | bytes 393220
  1.6 44.7 %copy-start.5 = (bf16[256,256]{1,0:T(8,128)(2,1)S(1)}, bf16[256,256]{1,0:T(8,128)(2,1)}, u32[]{:S(2)}) copy-start(bf16[256,256]{1,0:T(8,128)(2,1)} %wo_ref.1) | copy-start | bytes 393220
  1.6 44.7 %copy-start.6 = (f32[256]{0:T(256)S(1)}, f32[256]{0:T(256)}, u32[]{:S(2)}) copy-start(f32[256]{0:T(256)} %param.12) | copy-start | bytes 3076
  1.7 44.7 %copy-start.8 = (s32[6]{0:T(128)S(1)}, s32[6]{0:T(128)}, u32[]{:S(2)}) copy-start(s32[6]{0:T(128)} %counts_ref.1) | copy-start | bytes 76
  1.7 44.7 %copy-start.9 = (s32[6]{0:T(128)S(1)}, s32[6]{0:T(128)}, u32[]{:S(2)}) copy-start(s32[6]{0:T(128)} %offsets_ref.1) | copy-start | bytes 76
  57.7 40.7 %copy-start = (bf16[256,1024]{1,0:T(8,128)(2,1)S(1)}, bf16[256,1024]{1,0:T(8,128)(2,1)}, u32[]{:S(2)}) copy-start(bf16[256,1024]{1,0:T(8,128)(2,1)} %up_ref.1) | copy-start | bytes 1572868
  57.7 40.7 %copy-start.1 = (bf16[1024,256]{1,0:T(8,128)(2,1)S(1)}, bf16[1024,256]{1,0:T(8,128)(2,1)}, u32[]{:S(2)}) copy-start(bf16[1024,256]{1,0:T(8,128)(2,1)} %down_ref.1) | copy-start | bytes 1572868
  57.7 40.7 %copy-start.7 = (f32[256]{0:T(256)S(1)}, f32[256]{0:T(256)}, u32[]{:S(2)}) copy-start(f32[256]{0:T(256)} %param.17) | copy-start | bytes 3076

commit v3 on v2

--- a/solution.py
+++ b/solution.py
@@ -74,7 +74,6 @@
     out_ref[...] = x_ref[...]
 
     def place(m):
-        m = jnp.clip(m, 0, mixtures - 1)
         begin = offsets_ref[m]
         start = jnp.minimum(begin, slots - window)
         return start, begin - start, begin - start + counts_ref[m]
@@ -126,7 +125,6 @@
 
     def finish(m, q_ref, k_ref, v_ref, c_ref):
         start, low, high = place(m)
-        high = jnp.where(m < 0, low, high)
         for c in range(chunks):
             context = jnp.concatenate(
                 [c_ref[p, c * span : (c + 1) * span, :] for p in range(owned)], 0
@@ -138,19 +136,16 @@
             out_ref[pl.ds(start + c * span, span)] = middle.reshape(span, owned, width).astype(bf16)
 
     even, odd = held[:4], held[4:]
-    odd[3][...] = jnp.zeros(odd[3].shape, f32)
     project(0, *even)
 
-    def pair(i, carry):
-        m = 2 * i
-        for now, this, other in ((m, even, odd), (m + 1, odd, even)):
-            finish(now - 1, *other)
-            attend(now, *this)
-            project(now + 1, *other)
-        return carry
-
-    lax.fori_loop(0, pl.cdiv(mixtures, 2), pair, 0)
-    finish(2 * pl.cdiv(mixtures, 2) - 1, *odd)
+    for m in range(mixtures):
+        this, other = (odd, even) if m % 2 else (even, odd)
+        if m > 0:
+            finish(m - 1, *other)
+        attend(m, *this)
+        if m + 1 < mixtures:
+            project(m + 1, *other)
+    finish(mixtures - 1, *this)
 
 
 def attention(gathered, gain, w_query, w_key, w_value, w_out, counts, offsets):
@@ -173,14 +168,22 @@
     )(counts, offsets, gathered, gain, w_query, w_key, w_value, w_out)
 
 
-def feed_forward_kernel(each, x_ref, gain_ref, up_ref, down_ref, out_ref):
+def feed_forward_kernel(each, x_ref, gain_ref, up_ref, down_ref, out_ref, held_ref, sems):
     width = x_ref.shape[-1]
+    groups = held_ref.shape[0]
     gain = gain_ref[...]
-    for s in range(out_ref.shape[0]):
+
+    def leave(s):
+        return pltpu.make_async_copy(held_ref.at[s], out_ref.at[s], sems.at[s])
+
+    for s in range(groups):
         middle = x_ref[:, s * each : (s + 1) * each, :].astype(f32).reshape(-1, width)
         second = layer_norm(middle, gain)
         hidden = jnp.maximum(dot(second, up_ref[...]), 0.0).astype(bf16)
-        out_ref[s] = (middle + dot(hidden, down_ref[...])).astype(bf16)
+        held_ref[s] = (middle + dot(hidden, down_ref[...])).astype(bf16)
+        leave(s).start()
+    for s in range(groups):
+        leave(s).wait()
 
 
 def feed_forward(middle, groups, gain, w_up, w_down):
@@ -190,19 +193,14 @@
         middle = middle.reshape(devices, groups, each, width).swapaxes(0, 1)
         middle = middle.reshape(1, groups * devices * each, width)
         devices, each = 1, devices * each
-    block = 4 if groups % 4 == 0 else 1
-    whole = lambda shape: pl.BlockSpec(shape, lambda s: (0,) * len(shape))
+    vmem = pl.BlockSpec(memory_space=pltpu.VMEM)
+    shape = (groups, devices * each, width)
     return pl.pallas_call(
         functools.partial(feed_forward_kernel, each),
-        out_shape=jax.ShapeDtypeStruct((groups, devices * each, width), bf16),
-        grid=(groups // block,),
-        in_specs=[
-            pl.BlockSpec((devices, block * each, width), lambda s: (0, s, 0)),
-            whole(gain.shape),
-            whole(w_up.shape),
-            whole(w_down.shape),
-        ],
-        out_specs=pl.BlockSpec((block, devices * each, width), lambda s: (s, 0, 0)),
+        out_shape=jax.ShapeDtypeStruct(shape, bf16),
+        in_specs=[vmem] * 4,
+        out_specs=pl.BlockSpec(memory_space=pl.ANY),
+        scratch_shapes=[pltpu.VMEM(shape, bf16), pltpu.SemaphoreType.DMA((groups,))],
         compiler_params=pltpu.CompilerParams(vmem_limit_bytes=48 * 1024 * 1024),
         cost_estimate=pl.CostEstimate(
             flops=4 * middle.size * w_up.shape[1], bytes_accessed=4 * middle.size, transcendentals=0

time: 104 us -> 102 us (0.981)
  Pallas kernels: 17 us -> 14.6 us
    pallas_call x1, Pallas kernels: 11.3 us -> 9.96 us  [attention(): pl.pallas_call(functools.partial(attention_kernel, window), out_shape=jax...]
where the time goes in v3:
time: 102 us
  blocking collectives  85.3 us (84%)
  Pallas kernels  14.6 us (14%)
  local copies, waits for them, and re-layouts  1.65 us (2%)
    all_to_all x1, blocking collectives, local(): lax.all_to_all(sent, axes, split_axis=0, concat_axis=0, tiled=True)  44.6 us
    all_to_all x1, blocking collectives, local(): lax.all_to_all(middle, axes, split_axis=0, concat_axis=0, tiled=True)  40.7 us
    pallas_call x1, Pallas kernels, attention(): pl.pallas_call(functools.partial(attention_kernel, window), out_shape=jax...  9.96 us
    pallas_call x1, Pallas kernels, feed_forward(): pl.pallas_call(functools.partial(feed_forward_kernel, each), out_shape=ja...  4.69 us

profile of v3, /device:TPU:1, one launch (start us, length us, event | category | flops | bytes accessed | tf_op | source)
XLA Modules:
  0.0 101.9 jit_solution(5168180250136808901)
XLA Ops:
  0.0 1.6 %copy.12 = bf16[12,32,8,256]{3,2,0,1:T(8,128)(2,1)S(1)} copy(bf16[12,32,8,256]{3,2,1,0:T(8,128)(2,1)} %bitcast.11) | data formatting | bytes 3145728 | tf_op jit(solution)/shard_map/reshape | solution.py:220
  1.6 0.0 copy-start.2
  1.6 0.0 copy-start.3
  1.6 0.0 copy-start.4
  1.6 0.0 copy-start.5
  1.6 0.0 copy-start.6
  1.7 0.0 copy-start.8
  1.7 0.0 copy-start.9
  1.7 44.6 %all_to_all.10.x_ref = bf16[384,8,256]{2,1,0:T(8,128)(2,1)S(1)} all-to-all(bf16[384,8,256]{2,1,0:T(8,128)(2,1)S(1)} %bitcast.10), channel_id=1, replica_groups=mesh['group'=8,'pos'=4] {'group','pos'}, dimensions={0} | all-to-all | bytes 3145728 | tf_op jit(solution)/shard_map/all_to_all | solution.py:222
  46.3 0.0 copy-done.2
  46.3 0.0 copy-done.3
  46.3 0.0 copy-done.4
  46.3 0.0 copy-done.5
  46.3 0.0 copy-done.6
  46.3 0.0 copy-done.8
  46.4 0.0 copy-done.9
  46.4 10.0 %attention.1 = bf16[384,8,256]{2,1,0:T(8,128)(2,1)S(1)} custom-call(s32[6]{0:T(128)S(1)} %copy-done.8, s32[6]{0:T(128)S(1)} %copy-done.9, bf16[384,8,256]{2,1,0:T(8,128)(2,1)S(1)} %all_to_all.10.x_ref, f32[1,256]{1,0:T(1,128)S(1)} %bitcast.8, bf16[256,256]{1,0:T(8,128)(2,1)S(1)} %copy-done.2, bf16[256,256]{1,0:T(8,128)(2,1)S(1)} %copy-done.3, ...), custom_call_target="tpu_custom_call" | custom-call | flops 14000000000 | bytes 3145728 | tf_op jit(solution)/shard_map/attention/pallas_call | solution.py:157
  56.3 0.0 copy-start
  56.3 0.0 copy-start.1
  56.4 0.0 copy-start.7
  56.4 40.7 %all_to_all.11 = bf16[384,8,256]{2,1,0:T(8,128)(2,1)S(1)} all-to-all(bf16[384,8,256]{2,1,0:T(8,128)(2,1)S(1)} %attention.1), channel_id=1, replica_groups=mesh['group'=8,'pos'=4] {'group','pos'}, dimensions={0} | all-to-all | bytes 3145728 | tf_op jit(solution)/shard_map/all_to_all | solution.py:226
  97.1 0.0 copy-done
  97.1 0.0 copy-done.1
  97.1 0.0 copy-done.7
  97.1 4.7 %feed_forward.1 = bf16[12,256,256]{2,1,0:T(8,128)(2,1)} custom-call(bf16[32,96,256]{2,1,0:T(8,128)(2,1)S(1)} %bitcast.7, f32[1,256]{1,0:T(1,128)S(1)} %bitcast.9, bf16[256,1024]{1,0:T(8,128)(2,1)S(1)} %copy-done, bf16[1024,256]{1,0:T(8,128)(2,1)S(1)} %copy-done.1), custom_call_target="tpu_custom_call" | custom-call | flops 3221225472 | bytes 3145728 | tf_op jit(solution)/shard_map/feed_forward/pallas_call | solution.py:198
Async XLA Ops:
  1.6 44.7 %copy-start.2 = (bf16[256,256]{1,0:T(8,128)(2,1)S(1)}, bf16[256,256]{1,0:T(8,128)(2,1)}, u32[]{:S(2)}) copy-start(bf16[256,256]{1,0:T(8,128)(2,1)} %wq_ref.1) | copy-start | bytes 393220
  1.6 44.7 %copy-start.3 = (bf16[256,256]{1,0:T(8,128)(2,1)S(1)}, bf16[256,256]{1,0:T(8,128)(2,1)}, u32[]{:S(2)}) copy-start(bf16[256,256]{1,0:T(8,128)(2,1)} %wk_ref.1) | copy-start | bytes 393220
  1.6 44.7 %copy-start.4 = (bf16[256,256]{1,0:T(8,128)(2,1)S(1)}, bf16[256,256]{1,0:T(8,128)(2,1)}, u32[]{:S(2)}) copy-start(bf16[256,256]{1,0:T(8,128)(2,1)} %wv_ref.1) | copy-start | bytes 393220
  1.6 44.7 %copy-start.5 = (bf16[256,256]{1,0:T(8,128)(2,1)S(1)}, bf16[256,256]{1,0:T(8,128)(2,1)}, u32[]{:S(2)}) copy-start(bf16[256,256]{1,0:T(8,128)(2,1)} %wo_ref.1) | copy-start | bytes 393220
  1.6 44.7 %copy-start.6 = (f32[256]{0:T(256)S(1)}, f32[256]{0:T(256)}, u32[]{:S(2)}) copy-start(f32[256]{0:T(256)} %param.12) | copy-start | bytes 3076
  1.7 44.7 %copy-start.8 = (s32[6]{0:T(128)S(1)}, s32[6]{0:T(128)}, u32[]{:S(2)}) copy-start(s32[6]{0:T(128)} %counts_ref.1) | copy-start | bytes 76
  1.7 44.7 %copy-start.9 = (s32[6]{0:T(128)S(1)}, s32[6]{0:T(128)}, u32[]{:S(2)}) copy-start(s32[6]{0:T(128)} %offsets_ref.1) | copy-start | bytes 76
  56.3 40.7 %copy-start = (bf16[256,1024]{1,0:T(8,128)(2,1)S(1)}, bf16[256,1024]{1,0:T(8,128)(2,1)}, u32[]{:S(2)}) copy-start(bf16[256,1024]{1,0:T(8,128)(2,1)} %up_ref.1) | copy-start | bytes 1572868
  56.3 40.7 %copy-start.1 = (bf16[1024,256]{1,0:T(8,128)(2,1)S(1)}, bf16[1024,256]{1,0:T(8,128)(2,1)}, u32[]{:S(2)}) copy-start(bf16[1024,256]{1,0:T(8,128)(2,1)} %down_ref.1) | copy-start | bytes 1572868
  56.4 40.7 %copy-start.7 = (f32[256]{0:T(256)S(1)}, f32[256]{0:T(256)}, u32[]{:S(2)}) copy-start(f32[256]{0:T(256)} %param.17) | copy-start | bytes 3076
